TPU v7x, 256 devices: a whole 4x4x8 slice. The times are simulated.
256 devices in a mesh: dp: 4 (over y), expert: 64 (over x, z, core).
Axes of the slice: x: 4, y: 4, z: 8, core: 2. Of those that a mesh axis runs over, the one named last changes fastest.
Arguments:
- tokens: bfloat16 [32768, 4096], P(('dp', 'expert')), may hold values from -6 to 6
- routes: int32 [32768, 2], P(('dp', 'expert')), may hold values from 0 to 63, all different within a row; in each aligned block of 128 rows (0 to 127, 128 to 255, ...) at most 6 rows name the same one
- router_weight: bfloat16 [4096, 64], replicated, may hold values from -0.09375 to 0.09375
- shift: float32 [8, 4096], replicated, may hold values from -3 to 3
- scale: float32 [8, 4096], replicated, may hold values from -3 to 3
- gate_mod: float32 [8, 4096], replicated, may hold values from -4 to 4
- gate_weight: bfloat16 [64, 4096, 1024], P(None, ('dp', 'expert')), may hold values from -0.09375 to 0.09375
- up_weight: bfloat16 [64, 4096, 1024], P(None, ('dp', 'expert')), may hold values from -0.09375 to 0.09375
- down_weight: bfloat16 [64, 4096, 1024], P(None, ('dp', 'expert')), may hold values from -0.1875 to 0.1875
Outputs:
- update: bfloat16 [32768, 4096], P(('dp', 'expert'))
Inputs may be any that keep to these rules, and one draw needn't show every extreme that they name: `routes`: each row names two different experts; among the rows of one device no expert is named more than 6 times, a bound that some block reaches.
All inputs are finite; a program needn't handle non-finite values.
Results may differ from a plain program's by a relative error of at most 0.0072.
Values may be sent and summed in bfloat16 or wider, within the bound.
A program may use at most 128 MiB of HBM per device.

v0:
```python
import jax
import jax.numpy as jnp
from jax import lax
from jax.sharding import PartitionSpec as P

PIX = 4096


EPS = 1e-06


def send_back(output):
    return lax.all_to_all(output, "expert", split_axis=0, concat_axis=0, tiled=True)


def shards(
    tokens, routes, router_weight, shift, scale, gate_mod, gate_weight, up_weight, down_weight
):
    tok_dev = tokens.shape[0]
    width = tokens.shape[1]
    experts = router_weight.shape[1]
    n_owner = lax.axis_size("expert")
    local_count = experts // n_owner
    capacity = max(2, 3 * tok_dev // experts)
    first_row = (lax.axis_index("dp") * n_owner + lax.axis_index("expert")) * tok_dev
    image = first_row // PIX
    shift_row = lax.dynamic_slice_in_dim(shift, image, 1, 0)
    scale_row = lax.dynamic_slice_in_dim(scale, image, 1, 0)
    gate_row = lax.dynamic_slice_in_dim(gate_mod, image, 1, 0)
    values = tokens.astype(jnp.float32)
    meansq = jnp.mean(values * values, axis=-1, keepdims=True)
    normed = (values * lax.rsqrt(meansq + EPS) * (1.0 + scale_row) + shift_row).astype(jnp.bfloat16)
    logits = jnp.dot(normed, router_weight, preferred_element_type=jnp.float32)
    onehot = routes[:, :, None] == jnp.arange(experts, dtype=jnp.int32)[None, None, :]
    chosen = jnp.sum(jnp.where(onehot, logits[:, None, :], 0.0), axis=-1)
    score = jax.nn.sigmoid(chosen)
    flat = routes.reshape(-1)
    hot = (flat[:, None] == jnp.arange(experts, dtype=jnp.int32)[None, :]).astype(jnp.int32)
    rank = jnp.cumsum(hot, axis=0) - hot
    slot = jnp.sum(rank * hot, axis=-1)
    position = flat * capacity + slot
    source = (
        jnp.zeros((experts * capacity,), jnp.int32)
        .at[position]
        .set(jnp.arange(2 * tok_dev, dtype=jnp.int32) // 2)
    )
    filled = jnp.zeros((experts * capacity,), jnp.bool_).at[position].set(True)
    outgoing = jnp.where(filled[:, None], normed[source], jnp.zeros((), jnp.bfloat16)).reshape(
        experts, capacity, width
    )
    quarter_gate, quarter_up, quarter_down = (
        lax.all_to_all(gate_weight, "expert", split_axis=0, concat_axis=1, tiled=True),
        lax.all_to_all(up_weight, "expert", split_axis=0, concat_axis=1, tiled=True),
        lax.all_to_all(down_weight, "expert", split_axis=0, concat_axis=1, tiled=True),
    )
    w_gate, w_up, w_down = (
        lax.all_gather(quarter_gate, "dp", axis=1, tiled=True),
        lax.all_gather(quarter_up, "dp", axis=1, tiled=True),
        lax.all_gather(quarter_down, "dp", axis=1, tiled=True),
    )
    received = lax.all_to_all(outgoing, "expert", split_axis=0, concat_axis=0, tiled=True)
    slots = received.shape[1]
    grid = received.reshape(n_owner, local_count, slots, width)
    gate = jnp.einsum("nxcd,xdf->nxcf", grid, w_gate, preferred_element_type=jnp.float32)
    upper = jnp.einsum("nxcd,xdf->nxcf", grid, w_up, preferred_element_type=jnp.float32)
    hidden = (jax.nn.silu(gate) * upper).astype(jnp.bfloat16)
    output = jnp.einsum(
        "nxcf,xdf->nxcd", hidden, w_down, preferred_element_type=jnp.float32
    ).astype(jnp.bfloat16)
    output = output.reshape(n_owner * local_count, slots, width)
    incoming = send_back(output)
    picked = (
        incoming.reshape(experts * capacity, width)[position]
        .astype(jnp.float32)
        .reshape(tok_dev, 2, width)
    )
    branch = jnp.sum(score[:, :, None] * picked, axis=1)
    return (gate_row * branch).astype(jnp.bfloat16)


def solution(mesh):
    in_specs = (
        P(("dp", "expert"), None),
        P(("dp", "expert"), None),
        P(),
        P(),
        P(),
        P(),
        P(None, ("dp", "expert"), None),
        P(None, ("dp", "expert"), None),
        P(None, ("dp", "expert"), None),
    )
    out_specs = P(("dp", "expert"), None)
    return jax.shard_map(shards, mesh=mesh, in_specs=in_specs, out_specs=out_specs, check_vma=False)
```

profile of v0, /device:TPU:1, one launch (start us, length us, event | category | flops | bytes accessed | tf_op | source)
XLA Modules:
  0.0 491.7 jit_solution(17888451675752608027)
XLA Ops:
  6.5 64.4 %all_to_all.46 = bf16[64,16,1024]{2,1,0:T(8,128)(2,1)} all-to-all(bf16[64,16,1024]{2,1,0:T(8,128)(2,1)} %param.15), channel_id=1, replica_groups=mesh['dp'=4,'expert'=64] {'expert'}, dimensions={0} | all-to-all | bytes 4194304 | tf_op jit(solution)/shard_map/all_to_all | solution.py:52
  71.0 56.9 %all_to_all.47 = bf16[64,16,1024]{2,1,0:T(8,128)(2,1)} all-to-all(bf16[64,16,1024]{2,1,0:T(8,128)(2,1)S(1)} %copy-done.2), channel_id=1, replica_groups=mesh['dp'=4,'expert'=64] {'expert'}, dimensions={0} | all-to-all | bytes 4194304 | tf_op jit(solution)/shard_map/all_to_all | solution.py:53
  128.1 57.3 %all_to_all.48 = bf16[64,16,1024]{2,1,0:T(8,128)(2,1)} all-to-all(bf16[64,16,1024]{2,1,0:T(8,128)(2,1)} %param.17), channel_id=1, replica_groups=mesh['dp'=4,'expert'=64] {'expert'}, dimensions={0} | all-to-all | bytes 4194304 | tf_op jit(solution)/shard_map/all_to_all | solution.py:54
  185.8 0.6 reduce-window.6
  187.1 1.4 scatter_custom_fusion.1
  188.8 1.0 dynamic-slice_add_fusion
  190.2 4.0 gather_fusion
  194.2 5.7 %gather.9 = bf16[64,6,4096]{2,1,0:T(8,128)(2,1)} reshape(bf16[384,4096]{1,0:T(8,128)(2,1)} %gather_fusion) | data formatting | bytes 6291456 | tf_op jit(solution)/shard_map/gather | solution.py:48
  199.9 1.5 scatter_custom_fusion
  201.5 2.6 broadcast_select_fusion
  204.2 101.9 %all_to_all.49 = bf16[64,6,4096]{2,1,0:T(8,128)(2,1)} all-to-all(bf16[64,6,4096]{2,1,0:T(8,128)(2,1)S(1)} %broadcast_select_fusion), channel_id=1, replica_groups=mesh['dp'=4,'expert'=64] {'expert'}, dimensions={0} | all-to-all | bytes 6291456 | tf_op jit(solution)/shard_map/all_to_all | solution.py:61
  306.1 10.3 %fusion.4 = f32[64,6,1024]{2,0,1:T(8,128)} fusion(bf16[1,4096,1024]{2,1,0:T(8,128)(2,1)} %all-gather.4.cloned.1.call-done, bf16[64,6,4096]{2,1,0:T(8,128)(2,1)} %all_to_all.49), kind=kOutput, calls=%fused_computation.8 | convolution fusion | flops 3221225472 | bytes 13107200 | tf_op jit(solution)/shard_map/nxcd,xdf->nxcf/dot_general | solution.py:64
  316.4 13.8 %all-gather.8.cloned.1.call-done = bf16[1,4096,1024]{2,1,0:T(8,128)(2,1)} async-done(((bf16[1,1024,1024]{2,1,0:T(8,128)(2,1)}), bf16[1,4096,1024]{2,1,0:T(8,128)(2,1)}) %all-gather.8.cloned.1.call-update) | async-done | bytes 8388624 | tf_op jit(solution)/shard_map/all_gather | solution.py:59
  330.2 16.7 %fusion.6 = bf16[64,6,4096]{2,0,1:T(8,128)(2,1)} fusion(bf16[1,4096,1024]{2,1,0:T(8,128)(2,1)} %all-gather.8.cloned.1.call-done, bf16[1,4096,1024]{2,1,0:T(8,128)(2,1)} %all-gather.6.cloned.1.call-done, bf16[64,6,4096]{2,1,0:T(8,128)(2,1)} %all_to_all.49, f32[64,6,1024]{2,0,1:T(8,128)} %fusion.4), kind=kOutput, calls=%fused_computation.10 | convolution fusion | flops 6446383104 | bytes 24641536 | tf_op jit(solution)/shard_map/nxcf,xdf->nxcd/dot_general | solution.py:67
  346.8 5.6 %copy.37 = bf16[64,6,4096]{2,1,0:T(8,128)(2,1)} copy(bf16[64,6,4096]{2,0,1:T(8,128)(2,1)} %fusion.6) | data formatting | bytes 6291456 | tf_op jit(solution)/shard_map/convert_element_type | solution.py:69
  352.5 11.0 %all-to-all-start.4 = ((bf16[64,6,4096]{2,1,0:T(8,128)(2,1)}), bf16[64,6,4096]{2,1,0:T(8,128)(2,1)}, u32[]{:S(2)}, u32[]{:S(2)}) async-start(bf16[64,6,4096]{2,1,0:T(8,128)(2,1)} %copy.37), calls=%async_computation.4 | async-start | bytes 8388608 | tf_op jit(solution)/shard_map/all_to_all | solution.py:13
  363.5 0.5 fusion.42
  364.1 0.9 constant_dynamic-slice_fusion.1
  365.1 94.3 %all-to-all-done.4 = bf16[64,6,4096]{2,1,0:T(8,128)(2,1)} async-done(((bf16[64,6,4096]{2,1,0:T(8,128)(2,1)}), bf16[64,6,4096]{2,1,0:T(8,128)(2,1)}, u32[]{:S(2)}, u32[]{:S(2)}) %all-to-all-start.4) | async-done | bytes 3145760 | tf_op jit(solution)/shard_map/all_to_all | solution.py:13
  459.3 5.7 %reshape.113 = bf16[384,4096]{1,0:T(8,128)(2,1)} reshape(bf16[64,6,4096]{2,1,0:T(8,128)(2,1)} %all-to-all-done.4) | data formatting | bytes 6291456 | tf_op jit(solution)/shard_map/reshape | solution.py:73
  465.1 6.2 %gather_fusion.1 = bf16[256,4096]{1,0:T(8,128)(2,1)S(1)} fusion(bf16[384,4096]{1,0:T(8,128)(2,1)} %reshape.113, s32[1024]{0:T(1024)S(1)} %pad_clamp_fusion), kind=kCustom, calls=%fused_computation.1 | custom fusion | bytes 4195328 | tf_op jit(solution)/shard_map/gather | solution.py:73
  471.2 4.0 reshape.114
  475.2 8.7 %multiply_reduce_fusion = f32[128,4096]{1,0:T(8,128)S(1)} fusion(f32[128,2,4096]{2,1,0:T(2,128)} %reshape.114, f32[128,2]{1,0:T(8,128)S(1)} %copy.30), kind=kLoop, calls=%fused_computation.11 | loop fusion | flops 1572864 | bytes 6292480 | tf_op jit(solution)/shard_map/reduce_sum | solution.py:77
  484.0 1.1 multiply_convert_fusion
  (40 shorter events, 2.2 us)
Async XLA Ops:
  6.5 356.9 %copy-start = (bf16[4096,64]{0,1:T(8,128)(2,1)S(1)}, bf16[4096,64]{0,1:T(8,128)(2,1)}, u32[]{:S(2)}) copy-start(bf16[4096,64]{0,1:T(8,128)(2,1)} %param.11) | copy-start | bytes 1572868
  6.5 64.5 %copy-start.2 = (bf16[64,16,1024]{2,1,0:T(8,128)(2,1)S(1)}, bf16[64,16,1024]{2,1,0:T(8,128)(2,1)}, u32[]{:S(2)}) copy-start(bf16[64,16,1024]{2,1,0:T(8,128)(2,1)} %param.16) | copy-start | bytes 6291460
  6.5 299.6 %all-gather.4.cloned.1.call-start = ((), (), s32[]{:S(2)}) async-start(), calls=%async_computation.5 | async-start | bytes 10485760 | tf_op jit(solution)/shard_map/all_gather | solution.py:57
  71.0 245.4 %all-gather.6.cloned.1.call-start = ((), (), s32[]{:S(2)}) async-start(), calls=%async_computation.6 | async-start | bytes 10485760 | tf_op jit(solution)/shard_map/all_gather | solution.py:58
  128.0 57.4 %copy-start.3 = (s32[128,2]{0,1:T(2,128)S(1)}, s32[128,2]{0,1:T(2,128)}, u32[]{:S(2)}) copy-start(s32[128,2]{0,1:T(2,128)} %param.10) | copy-start | bytes 3076
  128.0 60.5 %copy-start.1 = (bf16[128,4096]{1,0:T(8,128)(2,1)S(1)}, bf16[128,4096]{1,0:T(8,128)(2,1)}, u32[]{:S(2)}) copy-start(bf16[128,4096]{1,0:T(8,128)(2,1)} %param.9) | copy-start | bytes 3145732
  128.0 202.1 %all-gather.8.cloned.1.call-start = ((), (), s32[]{:S(2)}) async-start(), calls=%async_computation.7 | async-start | bytes 10485760 | tf_op jit(solution)/shard_map/all_gather | solution.py:59
  352.5 106.9 %all-to-all-start.4 = ((bf16[64,6,4096]{2,1,0:T(8,128)(2,1)}), bf16[64,6,4096]{2,1,0:T(8,128)(2,1)}, u32[]{:S(2)}, u32[]{:S(2)}) async-start(bf16[64,6,4096]{2,1,0:T(8,128)(2,1)} %copy.37), calls=%async_computation.4 | async-start | bytes 8388608 | tf_op jit(solution)/shard_map/all_to_all | solution.py:13
Sparse Core Ops, SparseCore 0:
  71.1 82.1 all-gather.3
  155.1 86.5 all-gather.5
  243.5 86.5 all-gather.7
where the time goes:
time: 493 us; the launch traced here: 492 us
  blocking collectives  281 us (57%)
  waiting for transfers between devices  108 us (22%)
  local copies, waits for them, and re-layouts  36.1 us (7%)
  matrix products  27.5 us (6%)
  other arithmetic  15 us (3%)
  between operations  13.3 us (3%)
  starting transfers between devices  11.1 us (2%)
    all_to_all x1, blocking collectives, shards(): lax.all_to_all(outgoing, 'expert', split_axis=0, concat_axis=0, tiled=True)  102 us
    all_to_all x1, waiting for transfers between devices, send_back(): lax.all_to_all(output, 'expert', split_axis=0, concat_axis=0, tiled=True)  94.3 us
    all_to_all x1, blocking collectives, shards(): lax.all_to_all(gate_weight, 'expert', split_axis=0, concat_axis=1, tiled=...  64.4 us
    all_to_all x1, blocking collectives, shards(): lax.all_to_all(down_weight, 'expert', split_axis=0, concat_axis=1, tiled=...  57.3 us
    all_to_all x1, blocking collectives, shards(): lax.all_to_all(up_weight, 'expert', split_axis=0, concat_axis=1, tiled=True)  56.9 us
    dot_general x1, matrix products, shards(): jnp.einsum('nxcf,xdf->nxcd', hidden, w_down, preferred_element_type=jnp.f...  16.7 us
    all_gather x1, waiting for transfers between devices, shards(): lax.all_gather(quarter_down, 'dp', axis=1, tiled=True)  13.8 us
    all_to_all x1, starting transfers between devices, send_back(): lax.all_to_all(output, 'expert', split_axis=0, concat_axis=0, tiled=True)  11 us
  transfers between devices with their start and end apart: 4, of which 2 were waited for; matrix products, arithmetic and copies ran while one was open for 6% of the time, Pallas kernels for 0%

commit v1 on v0

v1 whole, which is shorter than its diff:
```python
import functools

import jax
import jax.numpy as jnp
import numpy as np
from jax import lax
from jax.experimental import pallas as pl
from jax.experimental.pallas import tpu as pltpu
from jax.sharding import PartitionSpec as P

MESH = pl.DeviceIdType.MESH
PIX = 4096
EPS = 1e-06
NX, NZ, NC, NY = 4, 8, 2, 4
N = NX * NZ * NC
CAP = 6
BLK = 512
NB = 8
ROWS = NB * CAP
GRP = 8
WIN = 16
LAG = 4
TLAG = 9
ROT = 20
F32, BF16 = jnp.float32, jnp.bfloat16


def offset(k):
    k = lax.rem(k + ROT, N)
    q, m = lax.div(k, 8), lax.rem(k, 8)
    dz = lax.rem(m * 5 + 4, NZ)
    dx = lax.rem(q + 2 * m + lax.div(m, 2), NX)
    dc = lax.rem(lax.div(q, 4) + m, NC)
    return dx, dz, dc


def kernel(
    tok, routes, router, shift, scale, gmod, perm, gate, up, down, out,
    W, NBUF, SB, RB, IB, XB, H, PICK, SCORE,
    sA, sP, sM, sR, sT, sO, sL, rA, rP, rM, rC, rT, rR,
):
    e = lax.axis_index("expert")
    y = lax.axis_index("dp")
    x, z, c = lax.div(e, NZ * NC), lax.rem(lax.div(e, NC), NZ), lax.rem(e, NC)
    yp, ym, y2 = lax.rem(y + 1, NY), lax.rem(y + 3, NY), lax.rem(y + 2, NY)

    def tgt(k):
        dx, dz, dc = offset(k)
        return (lax.rem(x + dx, NX) * NZ + lax.rem(z + dz, NZ)) * NC + lax.rem(c + dc, NC)

    def src(k):
        dx, dz, dc = offset(k)
        return (lax.rem(x + NX - dx, NX) * NZ + lax.rem(z + NZ - dz, NZ)) * NC + lax.rem(c + dc, NC)

    def loop(lo, hi, f):
        def body(k, carry):
            f(k)
            return carry
        lax.fori_loop(lo, hi, body, 0)

    bar = pltpu.get_barrier_semaphore()
    loop(1, N, lambda k: pl.semaphore_signal(bar, 1, device_id=(y, tgt(k)), device_id_type=MESH))
    pl.semaphore_signal(bar, 1, device_id=(yp, e), device_id_type=MESH)
    pl.semaphore_signal(bar, 1, device_id=(ym, e), device_id_type=MESH)
    pl.semaphore_wait(bar, N + 1)

    weights = (gate, up, down)

    def send_w(k):
        t = tgt(k)
        for j in range(3):
            pltpu.make_async_remote_copy(
                weights[j].at[t], W.at[y * N + e, j], sA, rA.at[k],
                device_id=(y, t), device_id_type=MESH,
            ).start()

    def chunk(i, s, r, device):
        return pltpu.make_async_remote_copy(
            W.at[i], W.at[i], s, r, device_id=device, device_id_type=MESH
        )

    def send_t(k):
        return pltpu.make_async_remote_copy(
            SB.at[k], RB.at[k], sT, rT.at[k], device_id=(y, tgt(k)), device_id_type=MESH
        )

    def send_o(k):
        return pltpu.make_async_remote_copy(
            SB.at[k], IB.at[k], sO, rR.at[k], device_id=(y, src(k)), device_id_type=MESH
        )

    for j in range(3):
        pltpu.make_async_copy(weights[j].at[e], W.at[y * N + e, j], sL).start()
    loop(1, WIN, send_w)

    image = lax.div((y * N + e) * tok.shape[0], PIX)
    square = jnp.zeros((tok.shape[0], 1), F32)
    for j in range(NB):
        v = tok[:, j * BLK:(j + 1) * BLK].astype(F32)
        square = square + jnp.sum(v * v, axis=-1, keepdims=True)
    inv = lax.rsqrt(square * (1.0 / (NB * BLK)) + EPS)
    logits = jnp.zeros((tok.shape[0], N), F32)
    for j in range(NB):
        cols = slice(j * BLK, (j + 1) * BLK)
        v = tok[:, cols].astype(F32)
        normed = v * inv * (1.0 + scale[pl.ds(image, 1), cols]) + shift[pl.ds(image, 1), cols]
        normed = normed.astype(BF16)
        NBUF[j] = normed
        logits = logits + jnp.dot(normed, router[cols, :], preferred_element_type=F32)
    tokens = tok.shape[0]
    experts = lax.broadcasted_iota(jnp.int32, (tokens, N), 1)
    named = [routes[:, k:k + 1] for k in range(2)]
    hot = [(experts == named[k]).astype(F32) for k in range(2)]
    below = (
        lax.broadcasted_iota(jnp.int32, (tokens, tokens), 1)
        < lax.broadcasted_iota(jnp.int32, (tokens, tokens), 0)
    ).astype(F32).astype(BF16)
    earlier = jnp.dot(below, (hot[0] + hot[1]).astype(BF16), preferred_element_type=F32)
    places = lax.broadcasted_iota(jnp.int32, (tokens, N * CAP), 1)
    both = None
    for k in range(2):
        r = named[k]
        ex, ez, ec = r >> 4, (r >> 1) & 7, r & 1
        dx, dz, dc = (ex - x + NX) & 3, (ez - z + NZ) & 7, (ec + c) & 1
        m = (dz * 5 + 4) & 7
        q = ((dx - 2 * m - (m >> 1) + 32) & 3) + 4 * ((dc + m) & 1)
        step = (8 * q + m + N - ROT) & (N - 1)
        slot = jnp.sum(hot[k] * earlier, axis=-1, keepdims=True).astype(jnp.int32)
        pick = (places == step * CAP + slot).astype(F32)
        PICK[k] = pick.astype(BF16)
        both = pick if both is None else both + pick
        chosen = jnp.sum(hot[k] * logits, axis=-1, keepdims=True)
        SCORE[k] = jnp.broadcast_to(jax.nn.sigmoid(chosen), (tokens, 128))
    select = both.T.astype(BF16)

    def gather_rows(j):
        XB[j] = jnp.dot(select, NBUF[j], preferred_element_type=F32).astype(BF16)
    loop(0, NB, gather_rows)

    def to_wire(g):
        rows = pl.ds(pl.multiple_of(g * ROWS, 16), ROWS)
        block = XB[:, rows, :].reshape(NB * ROWS, BLK)
        moved = jnp.dot(perm[...], block, preferred_element_type=F32).astype(BF16)
        SB[pl.ds(g * GRP, GRP)] = moved.reshape(GRP, ROWS, BLK)

    def from_wire(buf, g):
        rows = pl.ds(pl.multiple_of(g * ROWS, 16), ROWS)
        block = buf[pl.ds(g * GRP, GRP)].reshape(GRP * ROWS, BLK)
        moved = jnp.dot(perm[...], block, preferred_element_type=F32).astype(BF16)
        XB[:, rows, :] = moved.reshape(NB, ROWS, BLK)

    mine = W.at[y * N + e]
    pltpu.make_async_copy(mine, mine, sL).wait()

    def forward(k):
        i = y * N + src(k)
        chunk(i, sP, rP.at[k], (yp, e)).start()
        chunk(i, sM, rM.at[k], (ym, e)).start()

    def relay(k):
        s = src(k)

        def up_way():
            i = ym * N + s
            chunk(i, sP, rP.at[k], (yp, e)).wait_recv()
            chunk(i, sR, rC.at[k], (yp, e)).start()

        def down_way():
            i = yp * N + s
            chunk(i, sM, rM.at[k], (ym, e)).wait_recv()
            chunk(i, sR, rC.at[k], (ym, e)).start()

        lax.cond(lax.rem(k, 2) == 0, up_way, down_way)

    forward(0)

    def step(k):
        @pl.when(k + WIN - 1 < N)
        def _():
            send_w(k + WIN - 1)

        @pl.when(k <= N // GRP)
        def _():
            to_wire(k - 1)

        @pl.when(k > TLAG)
        def _():
            send_t(k - TLAG).start()

        chunk(y * N + src(k), sA, rA.at[k], (y, e)).wait_recv()
        forward(k)

        @pl.when(k >= LAG)
        def _():
            relay(k - LAG)

    loop(1, N, step)
    loop(N - TLAG, N, lambda k: send_t(k).start())
    loop(N - LAG, N, relay)
    RB[0] = SB[0]

    def last(k):
        s = src(k)

        def odd_way():
            chunk(yp * N + s, sM, rM.at[k], (ym, e)).wait_recv()

        def even_way():
            chunk(ym * N + s, sP, rP.at[k], (yp, e)).wait_recv()

        lax.cond(lax.rem(k, 2) == 0, odd_way, even_way)
        chunk(y2 * N + s, sR, rC.at[k], (yp, e)).wait_recv()

    loop(1, N, lambda k: send_t(k).wait_recv())
    loop(0, N // GRP, lambda g: from_wire(RB, g))
    loop(0, N, last)

    def hidden(n):
        cols = pl.ds(pl.multiple_of(n * 256, 256), 256)
        g = u = None
        for j in range(NB):
            rows = slice(j * 32, (j + 1) * 32)
            a = XB[j]
            pg = jnp.dot(a, W[rows, 0, :, cols].reshape(BLK, 256), preferred_element_type=F32)
            pu = jnp.dot(a, W[rows, 1, :, cols].reshape(BLK, 256), preferred_element_type=F32)
            g, u = (pg, pu) if g is None else (g + pg, u + pu)
        H[:, cols] = (g / (1.0 + jnp.exp(-g)) * u).astype(BF16)
    loop(0, 4, hidden)

    def outputs(j):
        wd = W[pl.ds(j * 32, 32), 2].reshape(BLK, 1024)
        o = lax.dot_general(H[...], wd, (((1,), (1,)), ((), ())), preferred_element_type=F32)
        XB[j] = o.astype(BF16)
    loop(0, NB, outputs)

    rest = SB.at[pl.ds(1, N - 1)]
    pltpu.make_async_remote_copy(rest, rest, sT, sL, device_id=(y, e), device_id_type=MESH).wait_send()

    def back(g):
        to_wire(g)

        @pl.when(g == 0)
        def _():
            IB[0] = SB[0]

        @pl.when(g > 0)
        def _():
            loop(0, GRP, lambda i: send_some(g * GRP - GRP + i))

    def send_some(k):
        @pl.when(k > 0)
        def _():
            send_o(k).start()

    loop(0, N // GRP, back)
    loop(N - GRP, N, lambda k: send_o(k).start())

    def come(g):
        def one(k):
            @pl.when(k > 0)
            def _():
                send_o(k).wait_recv()
        loop(g * GRP, g * GRP + GRP, one)
        from_wire(IB, g)

    loop(0, N // GRP, come)

    for j in range(NB):
        cols = slice(j * BLK, (j + 1) * BLK)
        block = XB[j]
        total = None
        for k in range(2):
            part = jnp.dot(PICK[k], block, preferred_element_type=F32) * SCORE[k][:, 0:1]
            total = part if total is None else total + part
        out[:, cols] = (gmod[pl.ds(image, 1), cols] * total).astype(BF16)

    pltpu.make_async_remote_copy(rest, rest, sO, sL, device_id=(y, e), device_id_type=MESH).wait_send()
    most = W.at[pl.ds(0, N - 1)]
    pltpu.make_async_remote_copy(most, most, sA, sL, device_id=(y, e), device_id_type=MESH).wait_send()
    full = W.at[pl.ds(0, N)]
    for s in (sP, sM, sR):
        pltpu.make_async_remote_copy(full, full, s, sL, device_id=(y, e), device_id_type=MESH).wait_send()


def permutation():
    p = np.zeros((NB * ROWS, GRP * ROWS), np.float32)
    for a in range(GRP):
        for j in range(NB):
            for r in range(CAP):
                p[a * ROWS + j * CAP + r, j * ROWS + a * CAP + r] = 1.0
    return p


def shards(tokens, routes, router_weight, shift, scale, gate_mod, gate_weight, up_weight, down_weight):
    rows, width = tokens.shape
    perm = jnp.asarray(permutation(), BF16)
    D = pltpu.SemaphoreType.DMA
    V = pltpu.VMEM
    vmem = pl.BlockSpec(memory_space=pltpu.VMEM)
    hbm = pl.BlockSpec(memory_space=pl.ANY)
    return pl.pallas_call(
        kernel,
        name="experts",
        out_shape=jax.ShapeDtypeStruct((rows, width), BF16),
        in_specs=[vmem] * 7 + [hbm] * 3,
        out_specs=vmem,
        scratch_shapes=[
            V((NY * N, 3, 16, 1024), BF16),
            V((NB, rows, BLK), BF16),
            V((N, ROWS, BLK), BF16),
            V((N, ROWS, BLK), BF16),
            V((N, ROWS, BLK), BF16),
            V((NB, N * CAP, BLK), BF16),
            V((N * CAP, 1024), BF16),
            V((2, rows, N * CAP), BF16),
            V((2, rows, 128), F32),
        ] + [D] * 7 + [D((N,))] * 6,
        compiler_params=pltpu.CompilerParams(
            collective_id=0, has_side_effects=True, vmem_limit_bytes=63 * 2**20
        ),
    )(tokens, routes, router_weight, shift, scale, gate_mod, perm, gate_weight, up_weight, down_weight)


def solution(mesh):
    spread = ("dp", "expert")
    in_specs = (
        P(spread, None), P(spread, None), P(), P(), P(), P(),
        P(None, spread, None), P(None, spread, None), P(None, spread, None),
    )
    return jax.shard_map(shards, mesh=mesh, in_specs=in_specs, out_specs=P(spread, None), check_vma=False)
```

time: 493 us -> 324 us (0.66)
  Pallas kernels: 0 us -> 317 us
  blocking collectives: 281 us -> 0 us
  waiting for transfers between devices: 108 us -> 0 us
  local copies, waits for them, and re-layouts: 36.1 us -> 6.04 us
  matrix products: 27.5 us -> 0 us
  other arithmetic: 15 us -> 0 us
  between operations: 13.3 us -> 0.01 us
  starting transfers between devices: 11.1 us -> 0 us
    pallas_call x0 -> x1, Pallas kernels: none -> 317 us  [shards(): pl.pallas_call(kernel, name='experts', out_shape=jax.ShapeDtypeStruct((ro...]
    all_to_all x4 -> x0, blocking collectives: 281 us -> none  [the longest x1 102 us: shards(): lax.all_to_all(outgoing, 'expert', split_axis=0, concat_axis=0, tiled=True)]
    all_to_all x1 -> x0, waiting for transfers between devices: 94.3 us -> none  [send_back(): lax.all_to_all(output, 'expert', split_axis=0, concat_axis=0, tiled=True)]
    dot_general x3 -> x0, matrix products: 27.5 us -> none  [the longest x1 16.7 us: shards(): jnp.einsum('nxcf,xdf->nxcd', hidden, w_down, preferred_element_type=jnp.f...]
    gather x3 -> x0, local copies, waits for them, and re-layouts: 15.9 us -> none  [the longest x2 9.69 us: shards(): normed[source]]
    all_gather x3 -> x0, waiting for transfers between devices: 13.8 us -> none  [the longest x1 13.8 us: shards(): lax.all_gather(quarter_down, 'dp', axis=1, tiled=True)]
    all_to_all x1 -> x0, starting transfers between devices: 11 us -> none  [send_back(): lax.all_to_all(output, 'expert', split_axis=0, concat_axis=0, tiled=True)]
    convert_element_type x2 -> x0, local copies, waits for them, and re-layouts: 9.61 us -> none  [the longest x1 5.61 us: shards(): output = jnp.einsum('nxcf,xdf->nxcd', hidden, w_down, preferred_element_t...]
  transfers between devices with their start and end apart: 4 -> 0, of which waited for: 2 -> 0; matrix products, arithmetic and copies ran while one was open for 6% -> 0% of each run, Pallas kernels for 0% -> 0%
where the time goes in v1:
time: 324 us; the launch traced here: 323 us
  Pallas kernels  317 us (98%)
  local copies, waits for them, and re-layouts  6.04 us (2%)
    pallas_call x1, Pallas kernels, shards(): pl.pallas_call(kernel, name='experts', out_shape=jax.ShapeDtypeStruct((ro...  317 us

profile of v1, /device:TPU:1, one launch (start us, length us, event | category | flops | bytes accessed | tf_op | source)
XLA Modules:
  0.0 323.5 jit_solution(15511258513845910227)
XLA Ops:
  0.0 1.4 copy.11.routes
  1.4 2.4 copy.12.router
  3.8 317.4 %experts.1 = bf16[128,4096]{1,0:T(8,128)(2,1)} custom-call(bf16[128,4096]{1,0:T(8,128)(2,1)} %tok.1, s32[128,2]{1,0:T(8,128)} %copy.11.routes, bf16[4096,64]{1,0:T(8,128)(2,1)} %copy.12.router, f32[8,4096]{1,0:T(8,128)} %shift.1, f32[8,4096]{1,0:T(8,128)} %scale.1, f32[8,4096]{1,0:T(8,128)} %gmod.1, bf16[384,384]{1,0:T(8,128)(2,1)} %constant.2.clone.perm, ...), custom_call_target="tpu_custom_call" | custom-call | tf_op jit(solution)/shard_map/experts/pallas_call | solution.py:301
  321.2 2.3 copy.14

commit v2 on v1

v2 whole, which is shorter than its diff:
```python
import functools

import jax
import jax.numpy as jnp
import numpy as np
from jax import lax
from jax.experimental import pallas as pl
from jax.experimental.pallas import tpu as pltpu
from jax.sharding import PartitionSpec as P

MESH = pl.DeviceIdType.MESH
PIX = 4096
EPS = 1e-06
NX, NZ, NC, NY = 4, 8, 2, 4
N = NX * NZ * NC
CAP = 6
BLK = 512
NB = 8
ROWS = NB * CAP
GRP = 8
NG = N // GRP
HALF = 256
NQ = NX * NZ
LAG = 4
ROT = 20
F32, BF16 = jnp.float32, jnp.bfloat16


def place(k):
    q = lax.rem(k + ROT, NQ)
    a, m = lax.div(q, 8), lax.rem(q, 8)
    dz = lax.rem(m * 5 + 4, NZ)
    dx = lax.rem(a + 2 * m + lax.div(m, 2), NX)
    return dx, dz, lax.div(k, NQ)


def kernel(
    tok_hbm, routes_hbm, router_hbm, shift_hbm, scale_hbm, gmod_hbm, perm_hbm, weave_hbm,
    gate, up, down, out,
    tok, routes, router, shift, scale, gmod, perm, weave, WG, WD, NBUF, SB, RB, XB, H, OUT, OB, IB, YB, PICK, SCORE, GP,
    sG, sGY, sD, sDY, sT, sO, sL, rG, rGP, rGM, rGR, rD, rDP, rDM, rDR, rT, rO, sI,
):
    e = lax.axis_index("expert")
    y = lax.axis_index("dp")
    x, z, c = lax.div(e, NZ * NC), lax.rem(lax.div(e, NC), NZ), lax.rem(e, NC)
    yp, ym, y2 = lax.rem(y + 1, NY), lax.rem(y + 3, NY), lax.rem(y + 2, NY)
    above, below = (yp, e), (ym, e)

    def chip(dx, dz):
        return lax.rem(x + dx, NX) * NZ + lax.rem(z + dz, NZ)

    def tgt(k):
        dx, dz, dc = place(k)
        return chip(dx, dz) * NC + lax.rem(c + dc, NC)

    def src(k):
        dx, dz, dc = place(k)
        return chip(NX - dx, NZ - dz) * NC + lax.rem(c + dc, NC)

    def loop(lo, hi, f):
        def body(k, carry):
            f(k)
            return carry
        lax.fori_loop(lo, hi, body, 0)

    def copy(a, b, s, r, device):
        return pltpu.make_async_remote_copy(a, b, s, r, device_id=device, device_id_type=MESH)

    bar = pltpu.get_barrier_semaphore()
    loop(1, N, lambda k: pl.semaphore_signal(bar, 1, device_id=(y, tgt(k)), device_id_type=MESH))
    pl.semaphore_signal(bar, 1, device_id=above, device_id_type=MESH)
    pl.semaphore_signal(bar, 1, device_id=below, device_id_type=MESH)
    small = (
        (tok_hbm, tok), (routes_hbm, routes), (router_hbm, router), (shift_hbm, shift),
        (scale_hbm, scale), (gmod_hbm, gmod), (perm_hbm, perm), (weave_hbm, weave),
    )
    loads = [pltpu.make_async_copy(a, b, sI.at[i]) for i, (a, b) in enumerate(small)]
    for load in loads:
        load.start()
    pl.semaphore_wait(bar, N + 1)

    def send_g(k):
        t = tgt(k)
        copy(gate.at[t], WG.at[y * N + e, 0], sG, rG.at[k], (y, t)).start()
        copy(up.at[t], WG.at[y * N + e, 1], sG, rG.at[k], (y, t)).start()

    mine_g = WG.at[y * N + e]
    mine_d = WD.at[c * NY * NQ + y * NQ + lax.div(e, NC)]
    pltpu.make_async_copy(gate.at[e], WG.at[y * N + e, 0], sL).start()
    pltpu.make_async_copy(up.at[e], WG.at[y * N + e, 1], sL).start()
    loop(1, N, send_g)
    pltpu.make_async_copy(mine_g, mine_g, sL).wait()
    pltpu.make_async_copy(down.at[e], mine_d, sL).start()

    def send_d(k):
        t = tgt(k)
        copy(down.at[t], mine_d, sD, rD.at[k], (y, t)).start()

    loop(1, NQ, send_d)
    pltpu.make_async_copy(mine_d, mine_d, sL).wait()

    for load in loads:
        load.wait()
    count = tok.shape[0]
    image = lax.div((y * N + e) * count, PIX)
    square = jnp.zeros((count, 1), F32)
    for j in range(NB):
        v = tok[:, j * BLK:(j + 1) * BLK].astype(F32)
        square = square + jnp.sum(v * v, axis=-1, keepdims=True)
    inv = lax.rsqrt(square * (1.0 / (NB * BLK)) + EPS)
    logits = jnp.zeros((count, N), F32)
    for j in range(NB):
        cols = slice(j * BLK, (j + 1) * BLK)
        v = tok[:, cols].astype(F32)
        normed = v * inv * (1.0 + scale[pl.ds(image, 1), cols]) + shift[pl.ds(image, 1), cols]
        normed = normed.astype(BF16)
        NBUF[j] = normed
        logits = logits + lax.dot_general(
            normed, router[:, cols], (((1,), (1,)), ((), ())), preferred_element_type=F32
        )
    experts = lax.broadcasted_iota(jnp.int32, (count, N), 1)
    tall = jnp.concatenate([routes[...].astype(F32), jnp.zeros((6, count), F32)], axis=0).T
    named = [tall[:, k:k + 1].astype(jnp.int32) for k in range(2)]
    hot = [(experts == named[k]).astype(F32) for k in range(2)]
    before = (
        lax.broadcasted_iota(jnp.int32, (count, count), 1)
        < lax.broadcasted_iota(jnp.int32, (count, count), 0)
    ).astype(F32).astype(BF16)
    earlier = jnp.dot(before, (hot[0] + hot[1]).astype(BF16), preferred_element_type=F32)
    places = lax.broadcasted_iota(jnp.int32, (count, N * CAP), 1)
    both = None
    for k in range(2):
        r = named[k]
        ex, ez, ec = r >> 4, (r >> 1) & 7, r & 1
        dx, dz, dc = (ex - x + NX) & 3, (ez - z + NZ) & 7, (ec + c) & 1
        m = (dz * 5 + 4) & 7
        a = (dx - 2 * m - (m >> 1) + 32) & 3
        step = ((8 * a + m + NQ - ROT) & (NQ - 1)) + NQ * dc
        slot = jnp.sum(hot[k] * earlier, axis=-1, keepdims=True).astype(jnp.int32)
        pick = (places == step * CAP + slot).astype(F32)
        PICK[k] = pick.astype(BF16)
        both = pick if both is None else both + pick
        chosen = jnp.sum(hot[k] * logits, axis=-1, keepdims=True)
        SCORE[k] = jnp.broadcast_to(jax.nn.sigmoid(chosen), (count, 128))
    select = both.T.astype(BF16)

    def gather_rows(j):
        XB[j] = jnp.dot(select, NBUF[j], preferred_element_type=F32).astype(BF16)
    loop(0, NB, gather_rows)

    for j in range(NB):
        left = gmod[pl.ds(image, 1), j * BLK:(j + 1) * BLK]
        terms = []
        for _ in range(3):
            term = left.astype(BF16)
            terms.append(term.astype(F32))
            left = left - terms[-1]
        stack = jnp.concatenate(terms + [jnp.zeros((5, BLK), F32)], axis=0).astype(BF16)
        moved = lax.dot_general(stack, weave[...], (((1,), (1,)), ((), ())), preferred_element_type=F32)
        GP[j:j + 1] = moved[0:1] + moved[1:2] + moved[2:3]

    def rows_of(g):
        return pl.ds(pl.multiple_of(g * ROWS, 16), ROWS)

    def turn(block):
        return jnp.dot(perm[...], block, preferred_element_type=F32).astype(BF16)

    def pack(g):
        block = turn(XB[:, rows_of(g), :].reshape(NB * ROWS, BLK))
        SB[pl.ds(g * GRP, GRP)] = block.reshape(GRP, ROWS, BLK)

    def unpack(g):
        block = turn(RB[pl.ds(g * GRP, GRP)].reshape(GRP * ROWS, BLK))
        XB[:, rows_of(g), :] = block.reshape(NB, ROWS, BLK)

    def send_t(k):
        copy(SB.at[k], RB.at[k], sT, rT.at[lax.div(k, GRP)], (y, tgt(k))).start()

    def forward_g(k):
        w = WG.at[y * N + src(k)]
        copy(w, w, sGY, rGP.at[k], above).start()
        copy(w, w, sGY, rGM.at[k], below).start()

    def up_g(k):
        w = WG.at[ym * N + src(k)]
        copy(w, w, sGY, rGP.at[k], above).wait_recv()
        return w

    def down_g(k):
        w = WG.at[yp * N + src(k)]
        copy(w, w, sGY, rGM.at[k], below).wait_recv()
        return w

    def far_g(k):
        w = WG.at[y2 * N + src(k)]
        copy(w, w, sGY, rGR.at[k], above).wait_recv()

    def relay_g(k):
        def one():
            w = up_g(k)
            copy(w, w, sGY, rGR.at[k], above).start()

        def two():
            w = down_g(k)
            copy(w, w, sGY, rGR.at[k], below).start()

        lax.cond(lax.rem(k, 2) == 0, one, two)

    def last_g(k):
        def one():
            down_g(k)

        def two():
            up_g(k)

        lax.cond(lax.rem(k, 2) == 0, one, two)
        far_g(k)

    forward_g(0)

    def step_g(k):
        @pl.when(k <= NG)
        def _():
            pack(k - 1)

        @pl.when((k >= 3) & (k < NG + 3))
        def _():
            first = (k - 3) * GRP
            loop(first, first + GRP, some_t)

        @pl.when(k == NG + 3)
        def _():
            loop(NQ, N, send_d)

        w = WG.at[y * N + src(k)]
        copy(w, w, sG, rG.at[k], above).wait_recv()
        forward_g(k)

        @pl.when(k >= LAG)
        def _():
            relay_g(k - LAG)

    def some_t(k):
        @pl.when(k > 0)
        def _():
            send_t(k)

    loop(1, N, step_g)
    loop(N - LAG, N, relay_g)
    RB[0] = SB[0]

    def class_of(phase):
        return lax.rem(c + phase, NC)

    def down_at(plane, k):
        return WD.at[class_of(lax.div(k, NQ)) * NY * NQ + plane * NQ + lax.div(src(k), NC)]

    def forward_d(k):
        w = down_at(y, k)

        @pl.when(k > 0)
        def _():
            copy(w, w, sD, rD.at[k], above).wait_recv()

        copy(w, w, sDY, rDP.at[k], above).start()
        copy(w, w, sDY, rDM.at[k], below).start()

    def up_d(k):
        w = down_at(ym, k)
        copy(w, w, sDY, rDP.at[k], above).wait_recv()
        return w

    def down_d(k):
        w = down_at(yp, k)
        copy(w, w, sDY, rDM.at[k], below).wait_recv()
        return w

    def relay_d(k):
        def one():
            w = up_d(k)
            copy(w, w, sDY, rDR.at[k], above).start()

        def two():
            w = down_d(k)
            copy(w, w, sDY, rDR.at[k], below).start()

        lax.cond(lax.rem(k, 2) == 0, one, two)

    def last_d(k):
        def one():
            down_d(k)

        def two():
            up_d(k)

        lax.cond(lax.rem(k, 2) == 0, one, two)
        w = down_at(y2, k)
        copy(w, w, sDY, rDR.at[k], above).wait_recv()

    def step_d(k):
        forward_d(k)

        @pl.when(k >= LAG)
        def _():
            relay_d(k - LAG)

    def hidden(n):
        cols = pl.ds(pl.multiple_of(n * 256, 256), 256)
        g = u = None
        for j in range(NB):
            rows = slice(j * 32, (j + 1) * 32)
            a = XB[j]
            pg = jnp.dot(a, WG[rows, 0, :, cols].reshape(BLK, 256), preferred_element_type=F32)
            pu = jnp.dot(a, WG[rows, 1, :, cols].reshape(BLK, 256), preferred_element_type=F32)
            g, u = (pg, pu) if g is None else (g + pg, u + pu)
        H[:, cols] = (g / (1.0 + jnp.exp(-g)) * u).astype(BF16)

    def send_o(kind, k):
        copy(
            OB.at[kind * N + k], IB.at[kind * N + k], sO,
            rO.at[kind * NG + lax.div(k, GRP)], (y, src(k)),
        ).start()

    def multiply(phase, also):
        kind = class_of(phase)

        def block(j):
            wd = WD[pl.ds(kind * NY * NQ + j * 16, 16)].reshape(HALF, 1024)
            o = lax.dot_general(H[...], wd, (((1,), (1,)), ((), ())), preferred_element_type=F32)
            OUT[j] = o.astype(BF16)
            also(j)
        loop(0, NB, block)

    def send_back(phase, also):
        kind = class_of(phase)

        def group(g):
            block = turn(OUT[:, rows_of(g), :].reshape(NB * ROWS, HALF))
            OB[pl.ds(kind * N + g * GRP, GRP)] = block.reshape(GRP, ROWS, HALF)

            @pl.when(g > 0)
            def _():
                loop(g * GRP - GRP, g * GRP, some)

            also(g)

        def some(k):
            @pl.when(k > 0)
            def _():
                send_o(kind, k)

        loop(0, NG, group)
        loop(N - GRP, N, some)
        IB[kind * N] = OB[kind * N]

    def collect(phase):
        def group(g):
            kind = lax.rem(c + phase + lax.div(g, NG // 2), NC)

            def wait(first, size):
                there = IB.at[pl.ds(kind * N + first, size)]
                copy(there, there, sO, rO.at[kind * NG + g], above).wait_recv()

            lax.cond(g == 0, lambda: wait(1, GRP - 1), lambda: wait(g * GRP, GRP))
            block = turn(IB[pl.ds(kind * N + g * GRP, GRP)].reshape(GRP * ROWS, HALF))
            YB[pl.ds(kind * NB, NB), rows_of(g), :] = block.reshape(NB, ROWS, HALF)
        loop(0, NG, group)

    def combine(j):
        parts = []
        for kind in range(NC):
            block = YB[kind * NB + j]
            total = None
            for k in range(2):
                part = jnp.dot(PICK[k], block, preferred_element_type=F32) * SCORE[k][:, 0:1]
                total = part if total is None else total + part
            parts.append((GP[j:j + 1, kind * HALF:(kind + 1) * HALF] * total).astype(BF16))
        both = jnp.concatenate(parts, axis=1)
        out[:, j * BLK:(j + 1) * BLK] = jnp.dot(both, weave[...], preferred_element_type=F32).astype(BF16)

    def hidden_and_pass(n):
        hidden(n)
        loop(NQ + 4 * n, NQ + 4 * n + 4, forward_d)

    def pass_more(j):
        forward_d(NQ + 16 + j)
        relay_d(NQ + j)

    def pass_most(g):
        forward_d(NQ + 24 + g)
        relay_d(NQ + 8 + g)

    def nothing(_):
        pass

    loop(0, NQ, step_d)
    loop(NQ - LAG, NQ, relay_d)
    for g in range(NG):
        there = RB.at[pl.ds(max(1, g * GRP), GRP - (g == 0))]
        copy(there, there, sT, rT.at[g], above).wait_recv()
    loop(0, NG, unpack)
    loop(0, N, last_g)
    loop(0, 4, hidden_and_pass)
    loop(0, NQ, last_d)
    multiply(0, pass_more)
    send_back(0, pass_most)
    loop(N - NQ // 2, N, relay_d)
    loop(NQ, N, last_d)
    multiply(1, nothing)
    send_back(1, nothing)
    collect(0)
    collect(1)
    for j in range(NB):
        combine(j)

    def left(ref, size, s):
        view = ref.at[pl.ds(0, size)]
        copy(view, view, s, sL, above).wait_send()

    left(WG, N - 1, sG)
    left(WG, 3 * N, sGY)
    left(WD, N - 1, sD)
    left(WD, 3 * N, sDY)
    left(SB, N - 1, sT)
    left(OB, 2 * N - 2, sO)


def permutation():
    p = np.zeros((NB * ROWS, GRP * ROWS), np.float32)
    for a in range(GRP):
        for j in range(NB):
            for r in range(CAP):
                p[a * ROWS + j * CAP + r, j * ROWS + a * CAP + r] = 1.0
    return p


def weaving():
    p = np.zeros((BLK, BLK), np.float32)
    for core in range(2):
        for s in range(16):
            for i in range(16):
                p[core * HALF + s * 16 + i, s * 32 + core * 16 + i] = 1.0
    return p


def shards(tokens, routes, router_weight, shift, scale, gate_mod, gate_weight, up_weight, down_weight):
    rows, width = tokens.shape
    perm, weave = jnp.asarray(permutation(), BF16), jnp.asarray(weaving(), BF16)
    small = (tokens, routes.T, router_weight.T, shift, scale, gate_mod, perm, weave)
    D = pltpu.SemaphoreType.DMA
    V = pltpu.VMEM
    vmem = pl.BlockSpec(memory_space=pltpu.VMEM)
    hbm = pl.BlockSpec(memory_space=pl.ANY)
    return pl.pallas_call(
        kernel,
        name="experts",
        out_shape=jax.ShapeDtypeStruct((rows, width), BF16),
        in_specs=[hbm] * 11,
        out_specs=vmem,
        scratch_shapes=[V(a.shape, a.dtype) for a in small] + [
            V((NY * N, 2, 16, 1024), BF16),
            V((NY * N, 16, 1024), BF16),
            V((NB, rows, BLK), BF16),
            V((N, ROWS, BLK), BF16),
            V((N, ROWS, BLK), BF16),
            V((NB, N * CAP, BLK), BF16),
            V((N * CAP, 1024), BF16),
            V((NB, N * CAP, HALF), BF16),
            V((2 * N, ROWS, HALF), BF16),
            V((2 * N, ROWS, HALF), BF16),
            V((2 * NB, N * CAP, HALF), BF16),
            V((2, rows, N * CAP), BF16),
            V((2, rows, 128), F32),
            V((NB, BLK), F32),
        ] + [D] * 7 + [D((N,))] * 8 + [D((NG,)), D((2 * NG,)), D((8,))],
        compiler_params=pltpu.CompilerParams(
            collective_id=0, has_side_effects=True, vmem_limit_bytes=63 * 2**20
        ),
    )(*small, gate_weight, up_weight, down_weight)


def solution(mesh):
    spread = ("dp", "expert")
    in_specs = (
        P(spread, None), P(spread, None), P(), P(), P(), P(),
        P(None, spread, None), P(None, spread, None), P(None, spread, None),
    )
    return jax.shard_map(shards, mesh=mesh, in_specs=in_specs, out_specs=P(spread, None), check_vma=False)
```

time: 324 us -> 298 us (0.920)
  Pallas kernels: 317 us -> 294 us
  local copies, waits for them, and re-layouts: 6.04 us -> 2.29 us
    pallas_call x1, Pallas kernels: 317 us -> 294 us  [shards(): pl.pallas_call(kernel, name='experts', out_shape=jax.ShapeDtypeStruct((ro...]
    unnamed x3 -> x1, local copies, waits for them, and re-layouts: 6.04 us -> 2.29 us
where the time goes in v2:
time: 298 us; the launch traced here: 296 us
  Pallas kernels  294 us (99%)
    pallas_call x1, Pallas kernels, shards(): pl.pallas_call(kernel, name='experts', out_shape=jax.ShapeDtypeStruct((ro...  294 us

profile of v2, /device:TPU:1, one launch (start us, length us, event | category | flops | bytes accessed | tf_op | source)
XLA Modules:
  0.0 296.1 jit_solution(11276202372846635449)
XLA Ops:
  0.0 293.8 %experts.1 = bf16[128,4096]{1,0:T(8,128)(2,1)} custom-call(bf16[128,4096]{1,0:T(8,128)(2,1)} %tok_hbm.1, s32[2,128]{1,0:T(2,128)} %bitcast.3, bf16[64,4096]{1,0:T(8,128)(2,1)} %bitcast.2, f32[8,4096]{1,0:T(8,128)} %shift_hbm.1, f32[8,4096]{1,0:T(8,128)} %scale_hbm.1, f32[8,4096]{1,0:T(8,128)} %gmod_hbm.1, bf16[384,384]{1,0:T(8,128)(2,1)} %constant.4.clone.perm_hbm, ...), custom_call_target="tpu_custom_call" | custom-call | tf_op jit(solution)/shard_map/experts/pallas_call | solution.py:454
  293.8 2.3 copy.13

commit v3 on v2

--- a/solution.py
+++ b/solution.py
@@ -37,8 +37,8 @@
 def kernel(
     tok_hbm, routes_hbm, router_hbm, shift_hbm, scale_hbm, gmod_hbm, perm_hbm, weave_hbm,
     gate, up, down, out,
-    tok, routes, router, shift, scale, gmod, perm, weave, WG, WD, NBUF, SB, RB, XB, H, OUT, OB, IB, YB, PICK, SCORE, GP,
-    sG, sGY, sD, sDY, sT, sO, sL, rG, rGP, rGM, rGR, rD, rDP, rDM, rDR, rT, rO, sI,
+    tok, routes, router, shift, scale, gmod, perm, weave, WG, WD, NBUF, SB, RB, XB, H, OUT, OB, IB, ACC, PICK, SCORE, GP, DONE,
+    sG, sGY, sD, sDY, sT, sO, sL, rG, rGP, rGM, rGR, rD, rDP, rDM, rDR, rT, rO, sI, sE,
 ):
     e = lax.axis_index("expert")
     y = lax.axis_index("dp")
@@ -67,7 +67,15 @@
         return pltpu.make_async_remote_copy(a, b, s, r, device_id=device, device_id_type=MESH)
 
     bar = pltpu.get_barrier_semaphore()
-    loop(1, N, lambda k: pl.semaphore_signal(bar, 1, device_id=(y, tgt(k)), device_id_type=MESH))
+
+    def hello(k):
+        b, a = lax.div(k, 8), lax.rem(k, 8)
+        half = lax.div(b + 1, 2)
+        dz = NZ // 2 + jnp.where(lax.rem(b, 2) == 0, half, -half)
+        there = chip(NX - 1 - lax.div(a, 2), dz) * NC + lax.rem(c + 1 - lax.rem(a, 2), NC)
+        pl.semaphore_signal(bar, 1, device_id=(y, there), device_id_type=MESH)
+
+    loop(0, N - 1, hello)
     pl.semaphore_signal(bar, 1, device_id=above, device_id_type=MESH)
     pl.semaphore_signal(bar, 1, device_id=below, device_id_type=MESH)
     small = (
@@ -128,6 +136,7 @@
     ).astype(F32).astype(BF16)
     earlier = jnp.dot(before, (hot[0] + hot[1]).astype(BF16), preferred_element_type=F32)
     places = lax.broadcasted_iota(jnp.int32, (count, N * CAP), 1)
+    near = lax.broadcasted_iota(jnp.int32, (count, ROWS), 1)
     both = None
     for k in range(2):
         r = named[k]
@@ -137,8 +146,10 @@
         a = (dx - 2 * m - (m >> 1) + 32) & 3
         step = ((8 * a + m + NQ - ROT) & (NQ - 1)) + NQ * dc
         slot = jnp.sum(hot[k] * earlier, axis=-1, keepdims=True).astype(jnp.int32)
-        pick = (places == step * CAP + slot).astype(F32)
-        PICK[k] = pick.astype(BF16)
+        spot = step * CAP + slot
+        pick = (places == spot).astype(F32)
+        for g in range(NG):
+            PICK[g, k * count:(k + 1) * count, :] = (near == spot - g * ROWS).astype(F32).astype(BF16)
         both = pick if both is None else both + pick
         chosen = jnp.sum(hot[k] * logits, axis=-1, keepdims=True)
         SCORE[k] = jnp.broadcast_to(jax.nn.sigmoid(chosen), (count, 128))
@@ -147,6 +158,10 @@
     def gather_rows(j):
         XB[j] = jnp.dot(select, NBUF[j], preferred_element_type=F32).astype(BF16)
     loop(0, NB, gather_rows)
+
+    def clear(j):
+        ACC[j] = jnp.zeros(ACC.shape[1:], F32)
+    loop(0, NC * NB, clear)
 
     for j in range(NB):
         left = gmod[pl.ds(image, 1), j * BLK:(j + 1) * BLK]
@@ -363,20 +378,21 @@
 
             lax.cond(g == 0, lambda: wait(1, GRP - 1), lambda: wait(g * GRP, GRP))
             block = turn(IB[pl.ds(kind * N + g * GRP, GRP)].reshape(GRP * ROWS, HALF))
-            YB[pl.ds(kind * NB, NB), rows_of(g), :] = block.reshape(NB, ROWS, HALF)
+            for j in range(NB):
+                rows = jnp.dot(PICK[g], block[j * ROWS:(j + 1) * ROWS], preferred_element_type=F32)
+                total = rows[:count] * SCORE[0][:, 0:1] + rows[count:] * SCORE[1][:, 0:1]
+                ACC[kind * NB + j] = ACC[kind * NB + j] + total
         loop(0, NG, group)
 
+    def deliver(j):
+        cols = slice(j * BLK, (j + 1) * BLK)
+        return pltpu.make_async_copy(DONE.at[:, cols], out.at[:, cols], sE.at[j])
+
     def combine(j):
-        parts = []
-        for kind in range(NC):
-            block = YB[kind * NB + j]
-            total = None
-            for k in range(2):
-                part = jnp.dot(PICK[k], block, preferred_element_type=F32) * SCORE[k][:, 0:1]
-                total = part if total is None else total + part
-            parts.append((GP[j:j + 1, kind * HALF:(kind + 1) * HALF] * total).astype(BF16))
+        halves = [slice(kind * HALF, (kind + 1) * HALF) for kind in range(NC)]
+        parts = [(GP[j:j + 1, halves[kind]] * ACC[kind * NB + j]).astype(BF16) for kind in range(NC)]
         both = jnp.concatenate(parts, axis=1)
-        out[:, j * BLK:(j + 1) * BLK] = jnp.dot(both, weave[...], preferred_element_type=F32).astype(BF16)
+        DONE[:, j * BLK:(j + 1) * BLK] = jnp.dot(both, weave[...], preferred_element_type=F32).astype(BF16)
 
     def hidden_and_pass(n):
         hidden(n)
@@ -412,6 +428,9 @@
     collect(1)
     for j in range(NB):
         combine(j)
+        deliver(j).start()
+    for j in range(NB):
+        deliver(j).wait()
 
     def left(ref, size, s):
         view = ref.at[pl.ds(0, size)]
@@ -449,14 +468,13 @@
     small = (tokens, routes.T, router_weight.T, shift, scale, gate_mod, perm, weave)
     D = pltpu.SemaphoreType.DMA
     V = pltpu.VMEM
-    vmem = pl.BlockSpec(memory_space=pltpu.VMEM)
     hbm = pl.BlockSpec(memory_space=pl.ANY)
     return pl.pallas_call(
         kernel,
         name="experts",
         out_shape=jax.ShapeDtypeStruct((rows, width), BF16),
         in_specs=[hbm] * 11,
-        out_specs=vmem,
+        out_specs=hbm,
         scratch_shapes=[V(a.shape, a.dtype) for a in small] + [
             V((NY * N, 2, 16, 1024), BF16),
             V((NY * N, 16, 1024), BF16),
@@ -468,11 +486,12 @@
             V((NB, N * CAP, HALF), BF16),
             V((2 * N, ROWS, HALF), BF16),
             V((2 * N, ROWS, HALF), BF16),
-            V((2 * NB, N * CAP, HALF), BF16),
-            V((2, rows, N * CAP), BF16),
+            V((2 * NB, rows, HALF), F32),
+            V((NG, 2 * rows, ROWS), BF16),
             V((2, rows, 128), F32),
             V((NB, BLK), F32),
-        ] + [D] * 7 + [D((N,))] * 8 + [D((NG,)), D((2 * NG,)), D((8,))],
+            V((rows, width), BF16),
+        ] + [D] * 7 + [D((N,))] * 8 + [D((NG,)), D((2 * NG,)), D((8,)), D((NB,))],
         compiler_params=pltpu.CompilerParams(
             collective_id=0, has_side_effects=True, vmem_limit_bytes=63 * 2**20
         ),

time: 298 us -> 294 us (0.987)
  Pallas kernels: 294 us -> 291 us
where the time goes in v3:
time: 294 us
  Pallas kernels  291 us (99%)
    pallas_call x1, Pallas kernels, shards(): pl.pallas_call(kernel, name='experts', out_shape=jax.ShapeDtypeStruct((ro...  291 us

profile of v3, /device:TPU:1, one launch (start us, length us, event | category | flops | bytes accessed | tf_op | source)
XLA Modules:
  0.0 293.6 jit_solution(12638310054586516582)
XLA Ops:
  0.0 291.3 %experts.1 = bf16[128,4096]{1,0:T(8,128)(2,1)} custom-call(bf16[128,4096]{1,0:T(8,128)(2,1)} %tok_hbm.1, s32[2,128]{1,0:T(2,128)} %bitcast.3, bf16[64,4096]{1,0:T(8,128)(2,1)} %bitcast.2, f32[8,4096]{1,0:T(8,128)} %shift_hbm.1, f32[8,4096]{1,0:T(8,128)} %scale_hbm.1, f32[8,4096]{1,0:T(8,128)} %gmod_hbm.1, bf16[384,384]{1,0:T(8,128)(2,1)} %constant.4.clone.perm_hbm, ...), custom_call_target="tpu_custom_call" | custom-call | tf_op jit(solution)/shard_map/experts/pallas_call | solution.py:472
  291.3 2.3 copy.13

commit v4 on v3

--- a/solution.py
+++ b/solution.py
@@ -38,7 +38,7 @@
     tok_hbm, routes_hbm, router_hbm, shift_hbm, scale_hbm, gmod_hbm, perm_hbm, weave_hbm,
     gate, up, down, out,
     tok, routes, router, shift, scale, gmod, perm, weave, WG, WD, NBUF, SB, RB, XB, H, OUT, OB, IB, ACC, PICK, SCORE, GP, DONE,
-    sG, sGY, sD, sDY, sT, sO, sL, rG, rGP, rGM, rGR, rD, rDP, rDM, rDR, rT, rO, sI, sE,
+    sG, sGY, sD, sDY, sT, sO, sL, rG, rGY, rD, rDY, rT, rO, sI, sE,
 ):
     e = lax.axis_index("expert")
     y = lax.axis_index("dp")
@@ -171,8 +171,15 @@
             terms.append(term.astype(F32))
             left = left - terms[-1]
         stack = jnp.concatenate(terms + [jnp.zeros((5, BLK), F32)], axis=0).astype(BF16)
-        moved = lax.dot_general(stack, weave[...], (((1,), (1,)), ((), ())), preferred_element_type=F32)
-        GP[j:j + 1] = moved[0:1] + moved[1:2] + moved[2:3]
+        for q in range(2):
+            moved = lax.dot_general(
+                stack[:, q * HALF:(q + 1) * HALF], weave[...], (((1,), (1,)), ((), ())),
+                preferred_element_type=F32,
+            )
+            moved = moved[0:1] + moved[1:2] + moved[2:3]
+            for kind in range(NC):
+                at = kind * HALF + q * 128
+                GP[j:j + 1, at:at + 128] = moved[:, kind * 128:(kind + 1) * 128]
 
     def rows_of(g):
         return pl.ds(pl.multiple_of(g * ROWS, 16), ROWS)
@@ -191,45 +198,38 @@
     def send_t(k):
         copy(SB.at[k], RB.at[k], sT, rT.at[lax.div(k, GRP)], (y, tgt(k))).start()
 
+    def above_slot(k, shared):
+        return k + lax.rem(k, 2) * (shared + 1 - k)
+
+    def below_slot(k, shared):
+        return shared + lax.rem(k, 2) * (k - shared)
+
     def forward_g(k):
         w = WG.at[y * N + src(k)]
-        copy(w, w, sGY, rGP.at[k], above).start()
-        copy(w, w, sGY, rGM.at[k], below).start()
-
-    def up_g(k):
-        w = WG.at[ym * N + src(k)]
-        copy(w, w, sGY, rGP.at[k], above).wait_recv()
-        return w
-
-    def down_g(k):
-        w = WG.at[yp * N + src(k)]
-        copy(w, w, sGY, rGM.at[k], below).wait_recv()
-        return w
-
-    def far_g(k):
-        w = WG.at[y2 * N + src(k)]
-        copy(w, w, sGY, rGR.at[k], above).wait_recv()
+        copy(w, w, sGY, rGY.at[above_slot(k, N)], above).start()
+        copy(w, w, sGY, rGY.at[below_slot(k, N)], below).start()
 
     def relay_g(k):
         def one():
-            w = up_g(k)
-            copy(w, w, sGY, rGR.at[k], above).start()
+            w = WG.at[ym * N + src(k)]
+            copy(w, w, sGY, rGY.at[k], above).wait_recv()
+            copy(w, w, sGY, rGY.at[N + 2], above).start()
 
         def two():
-            w = down_g(k)
-            copy(w, w, sGY, rGR.at[k], below).start()
+            w = WG.at[yp * N + src(k)]
+            copy(w, w, sGY, rGY.at[k], below).wait_recv()
+            copy(w, w, sGY, rGY.at[N + 2], below).start()
 
         lax.cond(lax.rem(k, 2) == 0, one, two)
 
-    def last_g(k):
-        def one():
-            down_g(k)
-
-        def two():
-            up_g(k)
-
-        lax.cond(lax.rem(k, 2) == 0, one, two)
-        far_g(k)
+    def arrived(ref, first, size, s):
+        w = ref.at[pl.ds(first, size)]
+        copy(w, w, sL, s, above).wait_recv()
+
+    def last_g():
+        arrived(WG, yp * N, N // 2, rGY.at[N])
+        arrived(WG, ym * N, N // 2, rGY.at[N + 1])
+        arrived(WG, y2 * N, N, rGY.at[N + 2])
 
     forward_g(0)
 
@@ -277,40 +277,30 @@
         def _():
             copy(w, w, sD, rD.at[k], above).wait_recv()
 
-        copy(w, w, sDY, rDP.at[k], above).start()
-        copy(w, w, sDY, rDM.at[k], below).start()
-
-    def up_d(k):
-        w = down_at(ym, k)
-        copy(w, w, sDY, rDP.at[k], above).wait_recv()
-        return w
-
-    def down_d(k):
-        w = down_at(yp, k)
-        copy(w, w, sDY, rDM.at[k], below).wait_recv()
-        return w
+        shared = N + 3 * lax.div(k, NQ)
+        copy(w, w, sDY, rDY.at[above_slot(k, shared)], above).start()
+        copy(w, w, sDY, rDY.at[below_slot(k, shared)], below).start()
 
     def relay_d(k):
+        shared = N + 3 * lax.div(k, NQ)
+
         def one():
-            w = up_d(k)
-            copy(w, w, sDY, rDR.at[k], above).start()
+            w = down_at(ym, k)
+            copy(w, w, sDY, rDY.at[k], above).wait_recv()
+            copy(w, w, sDY, rDY.at[shared + 2], above).start()
 
         def two():
-            w = down_d(k)
-            copy(w, w, sDY, rDR.at[k], below).start()
+            w = down_at(yp, k)
+            copy(w, w, sDY, rDY.at[k], below).wait_recv()
+            copy(w, w, sDY, rDY.at[shared + 2], below).start()
 
         lax.cond(lax.rem(k, 2) == 0, one, two)
 
-    def last_d(k):
-        def one():
-            down_d(k)
-
-        def two():
-            up_d(k)
-
-        lax.cond(lax.rem(k, 2) == 0, one, two)
-        w = down_at(y2, k)
-        copy(w, w, sDY, rDR.at[k], above).wait_recv()
+    def last_d(phase):
+        first, shared = class_of(phase) * NY * NQ, N + 3 * phase
+        arrived(WD, first + yp * NQ, NQ // 2, rDY.at[shared])
+        arrived(WD, first + ym * NQ, NQ // 2, rDY.at[shared + 1])
+        arrived(WD, first + y2 * NQ, NQ, rDY.at[shared + 2])
 
     def step_d(k):
         forward_d(k)
@@ -388,11 +378,18 @@
         cols = slice(j * BLK, (j + 1) * BLK)
         return pltpu.make_async_copy(DONE.at[:, cols], out.at[:, cols], sE.at[j])
 
-    def combine(j):
-        halves = [slice(kind * HALF, (kind + 1) * HALF) for kind in range(NC)]
-        parts = [(GP[j:j + 1, halves[kind]] * ACC[kind * NB + j]).astype(BF16) for kind in range(NC)]
-        both = jnp.concatenate(parts, axis=1)
-        DONE[:, j * BLK:(j + 1) * BLK] = jnp.dot(both, weave[...], preferred_element_type=F32).astype(BF16)
+    def combine(some):
+        stack = []
+        for j in some:
+            halves = [slice(kind * HALF, (kind + 1) * HALF) for kind in range(NC)]
+            parts = [(GP[j:j + 1, halves[kind]] * ACC[kind * NB + j]).astype(BF16) for kind in range(NC)]
+            for q in range(2):
+                stack.append(jnp.concatenate([part[:, q * 128:(q + 1) * 128] for part in parts], axis=1))
+        rows = jnp.dot(jnp.concatenate(stack, axis=0), weave[...], preferred_element_type=F32).astype(BF16)
+        for i, j in enumerate(some):
+            for q in range(2):
+                at, row = j * BLK + q * HALF, (2 * i + q) * count
+                DONE[:, at:at + HALF] = rows[row:row + count]
 
     def hidden_and_pass(n):
         hidden(n)
@@ -415,20 +412,21 @@
         there = RB.at[pl.ds(max(1, g * GRP), GRP - (g == 0))]
         copy(there, there, sT, rT.at[g], above).wait_recv()
     loop(0, NG, unpack)
-    loop(0, N, last_g)
+    last_g()
     loop(0, 4, hidden_and_pass)
-    loop(0, NQ, last_d)
+    last_d(0)
     multiply(0, pass_more)
     send_back(0, pass_most)
     loop(N - NQ // 2, N, relay_d)
-    loop(NQ, N, last_d)
+    last_d(1)
     multiply(1, nothing)
     send_back(1, nothing)
     collect(0)
     collect(1)
-    for j in range(NB):
-        combine(j)
+    for j in range(0, NB, 2):
+        combine((j, j + 1))
         deliver(j).start()
+        deliver(j + 1).start()
     for j in range(NB):
         deliver(j).wait()
 
@@ -454,11 +452,11 @@
 
 
 def weaving():
-    p = np.zeros((BLK, BLK), np.float32)
+    p = np.zeros((HALF, HALF), np.float32)
     for core in range(2):
-        for s in range(16):
+        for s in range(8):
             for i in range(16):
-                p[core * HALF + s * 16 + i, s * 32 + core * 16 + i] = 1.0
+                p[core * 128 + s * 16 + i, s * 32 + core * 16 + i] = 1.0
     return p
 
 
@@ -491,7 +489,7 @@
             V((2, rows, 128), F32),
             V((NB, BLK), F32),
             V((rows, width), BF16),
-        ] + [D] * 7 + [D((N,))] * 8 + [D((NG,)), D((2 * NG,)), D((8,)), D((NB,))],
+        ] + [D] * 7 + [D((N,)), D((N + 3,)), D((N,)), D((N + 6,))] + [D((NG,)), D((2 * NG,)), D((8,)), D((NB,))],
         compiler_params=pltpu.CompilerParams(
             collective_id=0, has_side_effects=True, vmem_limit_bytes=63 * 2**20
         ),

time: 294 us -> 291 us (0.990)
  no operation moved by 1% of the time
where the time goes in v4:
time: 291 us
  Pallas kernels  289 us (99%)
    pallas_call x1, Pallas kernels, shards(): pl.pallas_call(kernel, name='experts', out_shape=jax.ShapeDtypeStruct((ro...  289 us

profile of v4, /device:TPU:1, one launch (start us, length us, event | category | flops | bytes accessed | tf_op | source)
XLA Modules:
  0.0 291.3 jit_solution(2693645037260398922)
XLA Ops:
  0.0 289.0 %experts.1 = bf16[128,4096]{1,0:T(8,128)(2,1)} custom-call(bf16[128,4096]{1,0:T(8,128)(2,1)} %tok_hbm.1, s32[2,128]{1,0:T(2,128)} %bitcast.3, bf16[64,4096]{1,0:T(8,128)(2,1)} %bitcast.2, f32[8,4096]{1,0:T(8,128)} %shift_hbm.1, f32[8,4096]{1,0:T(8,128)} %scale_hbm.1, f32[8,4096]{1,0:T(8,128)} %gmod_hbm.1, bf16[384,384]{1,0:T(8,128)(2,1)} %constant.4.clone.perm_hbm, ...), custom_call_target="tpu_custom_call" | custom-call | tf_op jit(solution)/shard_map/experts/pallas_call | solution.py:470
  289.0 2.3 copy.13

commit v5 on v4

--- a/solution.py
+++ b/solution.py
@@ -29,7 +29,7 @@
 def place(k):
     q = lax.rem(k + ROT, NQ)
     a, m = lax.div(q, 8), lax.rem(q, 8)
-    dz = lax.rem(m * 5 + 4, NZ)
+    dz = lax.rem(m * 7 + 4, NZ)
     dx = lax.rem(a + 2 * m + lax.div(m, 2), NX)
     return dx, dz, lax.div(k, NQ)
 
@@ -68,14 +68,15 @@
 
     bar = pltpu.get_barrier_semaphore()
 
-    def hello(k):
-        b, a = lax.div(k, 8), lax.rem(k, 8)
-        half = lax.div(b + 1, 2)
-        dz = NZ // 2 + jnp.where(lax.rem(b, 2) == 0, half, -half)
-        there = chip(NX - 1 - lax.div(a, 2), dz) * NC + lax.rem(c + 1 - lax.rem(a, 2), NC)
-        pl.semaphore_signal(bar, 1, device_id=(y, there), device_id_type=MESH)
-
-    loop(0, N - 1, hello)
+    along_x = [lax.rem(x + d, NX) * (NZ * NC) for d in range(NX)]
+    along_z = [lax.rem(z + d, NZ) * NC for d in range(NZ)]
+    along_c = [lax.rem(c + d, NC) for d in range(NC)]
+    for dz in (4, 3, 5, 2, 6, 1, 7, 0):
+        for dx in (2, 1, 3, 0):
+            for dc in range(NC):
+                if dz or dx or dc:
+                    there = along_x[dx] + along_z[dz] + along_c[dc]
+                    pl.semaphore_signal(bar, 1, device_id=(y, there), device_id_type=MESH)
     pl.semaphore_signal(bar, 1, device_id=above, device_id_type=MESH)
     pl.semaphore_signal(bar, 1, device_id=below, device_id_type=MESH)
     small = (
@@ -142,7 +143,7 @@
         r = named[k]
         ex, ez, ec = r >> 4, (r >> 1) & 7, r & 1
         dx, dz, dc = (ex - x + NX) & 3, (ez - z + NZ) & 7, (ec + c) & 1
-        m = (dz * 5 + 4) & 7
+        m = (dz * 7 + 4) & 7
         a = (dx - 2 * m - (m >> 1) + 32) & 3
         step = ((8 * a + m + NQ - ROT) & (NQ - 1)) + NQ * dc
         slot = jnp.sum(hot[k] * earlier, axis=-1, keepdims=True).astype(jnp.int32)

time: 291 us -> 290 us (level)
  no operation moved by 1% of the time
where the time goes in v5:
time: 290 us; the launch traced here: 289 us
  Pallas kernels  287 us (99%)
    pallas_call x1, Pallas kernels, shards(): pl.pallas_call(kernel, name='experts', out_shape=jax.ShapeDtypeStruct((ro...  287 us

profile of v5, /device:TPU:1, one launch (start us, length us, event | category | flops | bytes accessed | tf_op | source)
XLA Modules:
  0.0 289.5 jit_solution(9660683014149239337)
XLA Ops:
  0.0 287.2 %experts.1 = bf16[128,4096]{1,0:T(8,128)(2,1)} custom-call(bf16[128,4096]{1,0:T(8,128)(2,1)} %tok_hbm.1, s32[2,128]{1,0:T(2,128)} %bitcast.3, bf16[64,4096]{1,0:T(8,128)(2,1)} %bitcast.2, f32[8,4096]{1,0:T(8,128)} %shift_hbm.1, f32[8,4096]{1,0:T(8,128)} %scale_hbm.1, f32[8,4096]{1,0:T(8,128)} %gmod_hbm.1, bf16[384,384]{1,0:T(8,128)(2,1)} %constant.4.clone.perm_hbm, ...), custom_call_target="tpu_custom_call" | custom-call | tf_op jit(solution)/shard_map/experts/pallas_call | solution.py:471
  287.2 2.3 copy.13

commit v6 on v5

--- a/solution.py
+++ b/solution.py
@@ -423,6 +423,15 @@
     multiply(1, nothing)
     send_back(1, nothing)
     collect(0)
+    def left(ref, size, s):
+        view = ref.at[pl.ds(0, size)]
+        copy(view, view, s, sL, above).wait_send()
+
+    left(WG, N - 1, sG)
+    left(WG, 3 * N, sGY)
+    left(WD, N - 1, sD)
+    left(WD, 3 * N, sDY)
+    left(SB, N - 1, sT)
     collect(1)
     for j in range(0, NB, 2):
         combine((j, j + 1))
@@ -431,15 +440,6 @@
     for j in range(NB):
         deliver(j).wait()
 
-    def left(ref, size, s):
-        view = ref.at[pl.ds(0, size)]
-        copy(view, view, s, sL, above).wait_send()
-
-    left(WG, N - 1, sG)
-    left(WG, 3 * N, sGY)
-    left(WD, N - 1, sD)
-    left(WD, 3 * N, sDY)
-    left(SB, N - 1, sT)
     left(OB, 2 * N - 2, sO)
 
 

time: 290 us -> 290 us (level)
  no operation moved by 1% of the time
where the time goes in v6:
time: 290 us; the launch traced here: 289 us
  Pallas kernels  287 us (99%)
    pallas_call x1, Pallas kernels, shards(): pl.pallas_call(kernel, name='experts', out_shape=jax.ShapeDtypeStruct((ro...  287 us

profile of v6, /device:TPU:1, one launch (start us, length us, event | category | flops | bytes accessed | tf_op | source)
XLA Modules:
  0.0 289.5 jit_solution(7064934891226222713)
XLA Ops:
  0.0 287.2 %experts.1 = bf16[128,4096]{1,0:T(8,128)(2,1)} custom-call(bf16[128,4096]{1,0:T(8,128)(2,1)} %tok_hbm.1, s32[2,128]{1,0:T(2,128)} %bitcast.3, bf16[64,4096]{1,0:T(8,128)(2,1)} %bitcast.2, f32[8,4096]{1,0:T(8,128)} %shift_hbm.1, f32[8,4096]{1,0:T(8,128)} %scale_hbm.1, f32[8,4096]{1,0:T(8,128)} %gmod_hbm.1, bf16[384,384]{1,0:T(8,128)(2,1)} %constant.4.clone.perm_hbm, ...), custom_call_target="tpu_custom_call" | custom-call | tf_op jit(solution)/shard_map/experts/pallas_call | solution.py:471
  287.2 2.3 copy.13
